TPU v7x, 32 devices: a whole 2x2x4 slice. The times are simulated.
32 devices in a mesh: dp: 8 (over z, x), txt: 4 (over y, core).
Axes of the slice: x: 2, y: 2, z: 4, core: 2. Of those that a mesh axis runs over, the one named last changes fastest.
Arguments:
- resid: bfloat16 [2048, 1024], P('dp', 'txt'), may hold values from -40 to 40
- prenorm_gain: float32 [1024], replicated, may hold values from 0.25 to 1.75
- prenorm_bias: float32 [1024], replicated, may hold values from -3 to 3
- up_weight: bfloat16 [1024, 4096], P('dp', 'txt'), may hold values from -0.1875 to 0.1875
- up_bias: float32 [4096], P('txt'), may hold values from -3 to 3
- down_weight: bfloat16 [4096, 1024], P('txt', 'dp'), may hold values from -0.09375 to 0.09375
- down_bias: float32 [1024], replicated, may hold values from -3 to 3
- post_gain: float32 [1024], P('txt'), may hold values from 0.25 to 1.75
- post_bias: float32 [1024], P('txt'), may hold values from -3 to 3
- projection: bfloat16 [1024, 768], P('txt'), may hold values from -1 to 1
- texts: bfloat16 [5120, 768], P('txt'), may hold values from -48 to 48
- labels: int32 [2048], P('dp'), may hold values from 0 to 5119
- step_size: float32 [1], replicated, may hold values from 0.5 to 2
Outputs:
- adversarial: float32 [2048, 1024], P('dp', 'txt')
All inputs are finite; a program needn't handle non-finite values.
Results may differ from a plain program's by a relative error of at most 0.0036.
Values may be sent and summed in bfloat16 or wider, within the bound.
A program may use at most 64 MiB of HBM per device.

v0:
```python
import jax
import jax.numpy as jnp
from jax import lax
from jax.sharding import PartitionSpec as P

MODEL_WIDTH = 1024


def local(
    resid,
    prenorm_gain,
    prenorm_bias,
    up_weight,
    up_bias,
    down_weight,
    down_bias,
    post_gain,
    post_bias,
    projection,
    texts,
    labels,
    step_size,
):
    feature_width = resid.shape[1]
    shift_amount = lax.axis_index("txt") * feature_width
    gathered = lax.all_gather(resid, "txt", axis=1, tiled=True)
    input_rows = gathered.astype(jnp.float32)
    input_mean = jnp.mean(input_rows, axis=1, keepdims=True)
    var_in = jnp.mean(input_rows * input_rows, axis=1, keepdims=True) - input_mean * input_mean
    input_inverse_deviation = lax.rsqrt(var_in + 1e-05)
    centered_input = (input_rows - input_mean) * input_inverse_deviation
    normed_input = (centered_input * prenorm_gain + prenorm_bias).astype(jnp.bfloat16)
    w_up = lax.all_gather(up_weight, "dp", axis=0, tiled=True)
    w_down = lax.all_gather(down_weight, "dp", axis=1, tiled=True)
    pre_act = jnp.dot(normed_input, w_up, preferred_element_type=jnp.float32) + up_bias
    gate_sig = jax.nn.sigmoid(1.702 * pre_act)
    hidden = (pre_act * gate_sig).astype(jnp.bfloat16)
    mixed_part = jnp.dot(hidden, w_down, preferred_element_type=jnp.float32)
    mixed = lax.psum_scatter(mixed_part, "txt", scatter_dimension=1, tiled=True)
    own_rows = resid.astype(jnp.float32)
    block_out = own_rows + mixed + lax.dynamic_slice_in_dim(down_bias, shift_amount, feature_width)
    out_sums = lax.psum((jnp.sum(block_out, axis=1), jnp.sum(block_out * block_out, axis=1)), "txt")
    mean_out = out_sums[0][:, None] / MODEL_WIDTH
    var_out = out_sums[1][:, None] / MODEL_WIDTH - mean_out * mean_out
    rstd_out = lax.rsqrt(var_out + 1e-05)
    yhat = (block_out - mean_out) * rstd_out
    post_normed = (yhat * post_gain + post_bias).astype(jnp.bfloat16)
    emb_part = jnp.dot(post_normed, projection, preferred_element_type=jnp.float32)
    embedding = lax.psum_scatter(emb_part, "txt", scatter_dimension=0, tiled=True)
    emb_norm = jnp.sqrt(jnp.sum(embedding * embedding, axis=1, keepdims=True) + 1e-06)
    unit_vec = embedding / emb_norm
    unit_low = lax.all_gather(unit_vec.astype(jnp.bfloat16), "txt", axis=0, tiled=True)
    text_f = texts.astype(jnp.float32)
    text_unit = (text_f / jnp.sqrt(jnp.sum(text_f * text_f, axis=1, keepdims=True) + 1e-06)).astype(
        jnp.bfloat16
    )
    logits = 100.0 * jnp.einsum(
        "ie,je->ij", unit_low, text_unit, preferred_element_type=jnp.float32
    )
    local_top = jnp.max(logits, axis=1)
    row_top = lax.pmax(local_top, "txt")
    exponent = jnp.exp(logits - row_top[:, None])
    row_total = lax.psum(jnp.sum(exponent, axis=1), "txt")
    prob = exponent / row_total[:, None]
    local_label = labels - lax.axis_index("txt") * texts.shape[0]
    columns = lax.broadcasted_iota(jnp.int32, logits.shape, 1)
    target = (columns == local_label[:, None]).astype(jnp.float32)
    score_grad = (100.0 * (prob - target)).astype(jnp.bfloat16)
    back_part = jnp.dot(score_grad, text_unit, preferred_element_type=jnp.float32)
    unit_grad = lax.psum_scatter(back_part, "txt", scatter_dimension=0, tiled=True)
    along = jnp.sum(unit_vec * unit_grad, axis=1, keepdims=True)
    grad_share = ((unit_grad - unit_vec * along) / emb_norm).astype(jnp.bfloat16)
    emb_grad = lax.all_gather(grad_share, "txt", axis=0, tiled=True)
    post_grad = jnp.einsum("ie,de->id", emb_grad, projection, preferred_element_type=jnp.float32)
    scaled = post_grad * post_gain
    back_sums = lax.psum((jnp.sum(scaled, axis=1), jnp.sum(scaled * yhat, axis=1)), "txt")
    output_gradient = (
        scaled - back_sums[0][:, None] / MODEL_WIDTH - yhat * (back_sums[1][:, None] / MODEL_WIDTH)
    ) * rstd_out
    out_full = lax.all_gather(output_gradient.astype(jnp.bfloat16), "txt", axis=1, tiled=True)
    hid_grad = jnp.einsum("id,fd->if", out_full, w_down, preferred_element_type=jnp.float32)
    act_grad = (hid_grad * (gate_sig + 1.702 * pre_act * gate_sig * (1.0 - gate_sig))).astype(
        jnp.bfloat16
    )
    normed_part = jnp.einsum("if,df->id", act_grad, w_up, preferred_element_type=jnp.float32)
    normed_gradient = lax.psum_scatter(normed_part, "txt", scatter_dimension=1, tiled=True)
    centered_input_portion = lax.dynamic_slice_in_dim(
        centered_input, shift_amount, feature_width, 1
    )
    scaled_input = normed_gradient * lax.dynamic_slice_in_dim(
        prenorm_gain, shift_amount, feature_width
    )
    input_row_sums = lax.psum(
        (jnp.sum(scaled_input, axis=1), jnp.sum(scaled_input * centered_input_portion, axis=1)),
        "txt",
    )
    input_gradient = (
        output_gradient
        + (
            scaled_input
            - input_row_sums[0][:, None] / MODEL_WIDTH
            - centered_input_portion * (input_row_sums[1][:, None] / MODEL_WIDTH)
        )
        * input_inverse_deviation
    )
    square_sum = lax.psum(jnp.sum(input_gradient * input_gradient, axis=1), "txt")
    grad_rms = jnp.sqrt(square_sum[:, None] / MODEL_WIDTH + 1e-06)
    return own_rows + step_size[0] * input_gradient / grad_rms


def solution(mesh):
    placed = (
        P("dp", "txt"),
        P(),
        P(),
        P("dp", "txt"),
        P("txt"),
        P("txt", "dp"),
        P(),
        P("txt"),
        P("txt"),
        P("txt", None),
        P("txt", None),
        P("dp"),
        P(),
    )
    return jax.shard_map(
        local, mesh=mesh, in_specs=placed, out_specs=P("dp", "txt"), check_vma=False
    )
```

profile of v0, /device:TPU:0, one launch (start us, length us, event | category | flops | bytes accessed | tf_op | source)
XLA Modules:
  0.0 297.3 jit_solution(12234471146780298693)
XLA Ops:
  8.1 8.9 %all_gather.18 = bf16[256,1024]{1,0:T(8,128)(2,1)S(1)} all-gather(bf16[256,256]{1,0:T(8,128)(2,1)} %param.13), channel_id=1, replica_groups=mesh['dp'=8,'txt'=4] {'txt'}, dimensions={1}, use_global_device_ids=true | all-gather | bytes 655360 | tf_op jit(solution)/shard_map/all_gather | solution.py:26
  17.2 44.1 %all-gather.3.cloned.1.call-done = bf16[1024,1024]{1,0:T(8,128)(2,1)} async-done(((bf16[128,1024]{1,0:T(8,128)(2,1)}), bf16[1024,1024]{1,0:T(8,128)(2,1)}) %all-gather.3.cloned.1.call-update) | async-done | bytes 2097168 | tf_op jit(solution)/shard_map/all_gather | solution.py:33
  61.3 2.4 convolution_add_fusion
  63.7 48.5 %all-gather.5.cloned.1.call-done = bf16[1024,1024]{1,0:T(8,128)(2,1)} async-done(((bf16[1024,128]{1,0:T(8,128)(2,1)}), bf16[1024,1024]{1,0:T(8,128)(2,1)}) %all-gather.5.cloned.1.call-update) | async-done | bytes 2097168 | tf_op jit(solution)/shard_map/all_gather | solution.py:34
  112.3 3.3 %fusion.17 = f32[256,1024]{1,0:T(8,128)} fusion(bf16[1024,1024]{1,0:T(8,128)(2,1)} %all-gather.5.cloned.1.call-done, f32[256,1024]{1,0:T(8,128)S(1)} %convolution_add_fusion), kind=kOutput, calls=%fused_computation.32 | convolution fusion | flops 538443776 | bytes 4194304 | tf_op jit(solution)/shard_map/dot_general | solution.py:38
  115.7 0.9 dynamic_slice.9
  116.6 22.2 %reduce-scatter.5.cloned.1.call-done = f32[256,256]{1,0:T(8,128)} async-done(((f32[256,1024]{1,0:T(8,128)}), f32[256,256]{1,0:T(8,128)}) %reduce-scatter.5.cloned.1.call-update) | async-done | bytes 262160 | tf_op jit(solution)/shard_map/reduce_scatter | solution.py:39
  138.7 1.1 fusion.38
  139.8 5.8 %all-reduce.2 = (f32[256]{0:T(256)S(1)}, f32[256]{0:T(256)S(1)}) all-reduce(f32[256]{0:T(256)S(1)} %get-tuple-element.12, f32[256]{0:T(256)S(1)} %get-tuple-element.11), channel_id=1, replica_groups=mesh['dp'=8,'txt'=4] {'txt'}, use_global_device_ids=true, to_apply=%region_6.0 | all-reduce | flops 512 | bytes 4096 | tf_op jit(solution)/shard_map/psum | solution.py:42
  145.6 1.2 fusion.25
  147.4 1.7 fusion.1
  149.2 21.7 %reduce-scatter.7.cloned.1.call-done = f32[64,768]{1,0:T(8,128)} async-done(((f32[256,768]{1,0:T(8,128)}), f32[64,768]{1,0:T(8,128)}) %reduce-scatter.7.cloned.1.call-update) | async-done | bytes 196624 | tf_op jit(solution)/shard_map/reduce_scatter | solution.py:49
  170.9 1.0 multiply_reduce_fusion.6
  171.9 1.0 fusion.35
  173.0 6.1 %all_gather.21 = bf16[256,768]{1,0:T(8,128)(2,1)S(1)} all-gather(bf16[64,768]{1,0:T(8,128)(2,1)S(1)} %fusion.35), channel_id=1, replica_groups=mesh['dp'=8,'txt'=4] {'txt'}, dimensions={0}, use_global_device_ids=true | all-gather | bytes 491520 | tf_op jit(solution)/shard_map/all_gather | solution.py:52
  179.1 3.5 %fusion.41 = (f32[256]{0:T(256)S(1)}, f32[256,1280]{1,0:T(8,128)}) fusion(bf16[256,768]{1,0:T(8,128)(2,1)S(1)} %all_gather.21, bf16[1280,768]{1,0:T(8,128)(2,1)} %fusion.1), kind=kOutput, calls=%fused_computation.81 | convolution fusion | flops 503971584 | bytes 3671040 | tf_op jit(solution)/shard_map/ie,je->ij/dot_general | solution.py:57
  182.6 6.4 %pmax.7 = f32[256]{0:T(256)S(1)} all-reduce(f32[256]{0:T(256)S(1)} %get-tuple-element.28), channel_id=1, replica_groups=mesh['dp'=8,'txt'=4] {'txt'}, use_global_device_ids=true, to_apply=%region_11.0 | all-reduce | flops 256 | bytes 2048 | tf_op jit(solution)/shard_map/pmax | solution.py:61
  189.0 1.6 fusion.3
  190.7 5.7 %psum.58 = f32[256]{0:T(256)S(1)} all-reduce(f32[256]{0:T(256)S(1)} %fusion.3), channel_id=1, replica_groups=mesh['dp'=8,'txt'=4] {'txt'}, use_global_device_ids=true, to_apply=%region_13.0 | all-reduce | flops 256 | bytes 2048 | tf_op jit(solution)/shard_map/psum | solution.py:63
  196.3 3.2 %fusion.12 = f32[256,768]{1,0:T(8,128)} fusion(bf16[1280,768]{1,0:T(8,128)(2,1)S(1)} %copy-done.2, f32[256,1280]{1,0:T(8,128)} %get-tuple-element.29, s32[256]{0:T(256)S(1)} %broadcast_subtract_fusion, f32[256]{0:T(256)S(1)} %psum.58, f32[256]{0:T(256)S(1)} %pmax.7), kind=kOutput, calls=%fused_computation.27 | convolution fusion | flops 505610240 | bytes 4066304 | tf_op jit(solution)/shard_map/dot_general | solution.py:69
  199.6 23.9 %reduce-scatter.9.cloned.1.call-done = f32[64,768]{1,0:T(8,128)} async-done(((f32[256,768]{1,0:T(8,128)}), f32[64,768]{1,0:T(8,128)}) %reduce-scatter.9.cloned.1.call-update) | async-done | bytes 196624 | tf_op jit(solution)/shard_map/reduce_scatter | solution.py:70
  223.5 1.1 multiply_reduce_fusion.5
  224.6 1.1 divide_convert_fusion
  225.8 6.1 %all_gather.22 = bf16[256,768]{1,0:T(8,128)(2,1)S(1)} all-gather(bf16[64,768]{1,0:T(8,128)(2,1)S(1)} %divide_convert_fusion), channel_id=1, replica_groups=mesh['dp'=8,'txt'=4] {'txt'}, dimensions={0}, use_global_device_ids=true | all-gather | bytes 491520 | tf_op jit(solution)/shard_map/all_gather | solution.py:73
  232.3 6.5 %all-reduce.1 = (f32[256]{0:T(256)S(1)}, f32[256]{0:T(256)S(1)}) all-reduce(f32[256]{0:T(256)S(1)} %get-tuple-element.10, f32[256]{0:T(256)S(1)} %get-tuple-element.9), channel_id=1, replica_groups=mesh['dp'=8,'txt'=4] {'txt'}, use_global_device_ids=true, to_apply=%region_19.0 | all-reduce | flops 512 | bytes 4096 | tf_op jit(solution)/shard_map/psum | solution.py:76
  239.0 6.9 %all_gather.23 = bf16[256,1024]{1,0:T(8,128)(2,1)S(1)} all-gather(bf16[256,256]{1,0:T(8,128)(2,1)S(1)} %get-tuple-element.21), channel_id=1, replica_groups=mesh['dp'=8,'txt'=4] {'txt'}, dimensions={1}, use_global_device_ids=true | all-gather | bytes 655360 | tf_op jit(solution)/shard_map/all_gather | solution.py:80
  245.9 4.7 %fusion.4 = f32[256,1024]{1,0:T(8,128)} fusion(bf16[1024,1024]{1,0:T(8,128)(2,1)} %all-gather.3.cloned.1.call-done, bf16[256,1024]{1,0:T(8,128)(2,1)S(1)} %all_gather.23, bf16[1024,1024]{1,0:T(8,128)(2,1)} %all-gather.5.cloned.1.call-done, f32[256,1024]{1,0:T(8,128)S(1)} %copy-done.9), kind=kOutput, calls=%fused_computation.16 | convolution fusion | flops 1076363264 | bytes 6815744 | tf_op jit(solution)/shard_map/if,df->id/dot_general | solution.py:85
  252.3 23.6 %reduce-scatter.11.cloned.1.call-done = f32[256,256]{1,0:T(8,128)} async-done(((f32[256,1024]{1,0:T(8,128)}), f32[256,256]{1,0:T(8,128)}) %reduce-scatter.11.cloned.1.call-update) | async-done | bytes 262160 | tf_op jit(solution)/shard_map/reduce_scatter | solution.py:86
  275.8 1.1 multiply_reduce_fusion.4
  276.9 5.8 %all-reduce = (f32[256]{0:T(256)S(1)}, f32[256]{0:T(256)S(1)}) all-reduce(f32[256]{0:T(256)S(1)} %get-tuple-element.8, f32[256]{0:T(256)S(1)} %get-tuple-element.7), channel_id=1, replica_groups=mesh['dp'=8,'txt'=4] {'txt'}, use_global_device_ids=true, to_apply=%region_24.0 | all-reduce | flops 512 | bytes 4096 | tf_op jit(solution)/shard_map/psum | solution.py:93
  282.7 1.2 multiply_reduce_fusion
  283.9 5.7 %psum.63 = f32[256]{0:T(256)S(1)} all-reduce(f32[256]{0:T(256)S(1)} %get-tuple-element.19), channel_id=1, replica_groups=mesh['dp'=8,'txt'=4] {'txt'}, use_global_device_ids=true, to_apply=%region_26.0 | all-reduce | flops 256 | bytes 2048 | tf_op jit(solution)/shard_map/psum | solution.py:106
  (48 shorter events, 4.9 us)
Async XLA Ops:
  6.5 139.1 %copy-start = (bf16[256,768]{1,0:T(8,128)(2,1)S(1)}, bf16[256,768]{1,0:T(8,128)(2,1)}, u32[]{:S(2)}) copy-start(bf16[256,768]{1,0:T(8,128)(2,1)} %param.22) | copy-start | bytes 1179652
  6.5 54.8 %all-gather.3.cloned.1.call-start = ((), (), s32[]{:S(2)}) async-start(), calls=%async_computation.4 | async-start | bytes 2359296 | tf_op jit(solution)/shard_map/all_gather | solution.py:33
  7.3 105.0 %all-gather.5.cloned.1.call-start = ((), (), s32[]{:S(2)}) async-start(), calls=%async_computation.5 | async-start | bytes 2359296 | tf_op jit(solution)/shard_map/all_gather | solution.py:34
  8.0 130.7 %reduce-scatter.5.cloned.1.call-start = ((), (), s32[]{:S(2)}) async-start(), calls=%async_computation.6 | async-start | bytes 1310720 | tf_op jit(solution)/shard_map/reduce_scatter | solution.py:39
  63.7 51.9 %copy-start.8 = (f32[256,1024]{1,0:T(8,128)}, f32[256,1024]{1,0:T(8,128)S(1)}, u32[]{:S(2)}) copy-start(f32[256,1024]{1,0:T(8,128)S(1)} %convolution_add_fusion) | copy-start | bytes 3145732
  63.7 75.0 %copy-start.4 = (bf16[256,256]{1,0:T(8,128)(2,1)S(1)}, bf16[256,256]{1,0:T(8,128)(2,1)}, u32[]{:S(2)}) copy-start(bf16[256,256]{1,0:T(8,128)(2,1)} %param.13) | copy-start | bytes 393220
  63.7 81.9 %copy-start.5 = (f32[256]{0:T(256)S(1)}, f32[256]{0:T(256)}, u32[]{:S(2)}) copy-start(f32[256]{0:T(256)} %param.20) | copy-start | bytes 3076
  63.7 81.9 %copy-start.7 = (f32[256]{0:T(256)S(1)}, f32[256]{0:T(256)}, u32[]{:S(2)}) copy-start(f32[256]{0:T(256)} %param.21) | copy-start | bytes 3076
  115.6 31.4 %copy-start.6 = (s32[256]{0:T(256)S(1)}, s32[256]{0:T(256)}, u32[]{:S(2)}) copy-start(s32[256]{0:T(256)} %param.24) | copy-start | bytes 3076
  115.6 31.4 %copy-start.1 = (bf16[1280,768]{1,0:T(8,128)(2,1)S(1)}, bf16[1280,768]{1,0:T(8,128)(2,1)}, u32[]{:S(2)}) copy-start(bf16[1280,768]{1,0:T(8,128)(2,1)} %param.23) | copy-start | bytes 5898244
  115.6 55.3 %reduce-scatter.7.cloned.1.call-start = ((), (), s32[]{:S(2)}) async-start(), calls=%async_computation.7 | async-start | bytes 983040 | tf_op jit(solution)/shard_map/reduce_scatter | solution.py:49
  146.9 76.6 %reduce-scatter.9.cloned.1.call-start = ((), (), s32[]{:S(2)}) async-start(), calls=%async_computation.8 | async-start | bytes 983040 | tf_op jit(solution)/shard_map/reduce_scatter | solution.py:70
  179.1 17.2 %copy-start.2 = (bf16[1280,768]{1,0:T(8,128)(2,1)S(1)}, bf16[1280,768]{1,0:T(8,128)(2,1)}, u32[]{:S(2)}) copy-start(bf16[1280,768]{1,0:T(8,128)(2,1)} %fusion.1) | copy-start | bytes 5898244
  196.3 27.2 %copy-start.3 = (f32[64,768]{1,0:T(8,128)S(1)}, f32[64,768]{1,0:T(8,128)}, u32[]{:S(2)}) copy-start(f32[64,768]{1,0:T(8,128)} %reduce-scatter.7.cloned.1.call-done) | copy-start | bytes 589828
  199.5 76.3 %reduce-scatter.11.cloned.1.call-start = ((), (), s32[]{:S(2)}) async-start(), calls=%async_computation.9 | async-start | bytes 1310720 | tf_op jit(solution)/shard_map/reduce_scatter | solution.py:86
  224.6 21.2 %copy-start.9 = (f32[256,1024]{1,0:T(8,128)S(1)}, f32[256,1024]{1,0:T(8,128)}, u32[]{:S(2)}) copy-start(f32[256,1024]{1,0:T(8,128)} %copy-done.8) | copy-start | bytes 3145732
Sparse Core Ops, SparseCore 0:
  9.5 51.8 all-gather.2
  63.4 48.8 all-gather.4
  115.7 22.9 reduce-scatter.4
  147.0 23.8 reduce-scatter.6
  199.6 23.8 reduce-scatter.8
  250.7 25.0 reduce-scatter.10
where the time goes:
time: 298 us; the launch traced here: 297 us
  waiting for transfers between devices  185 us (62%)
  blocking collectives  63.8 us (21%)
  matrix products  18.7 us (6%)
  between operations  14.3 us (5%)
  other arithmetic  13.1 us (4%)
    all_gather x1, waiting for transfers between devices, local(): w_down = lax.all_gather(down_weight, 'dp', axis=1, tiled=True)  48.5 us
    all_gather x1, waiting for transfers between devices, local(): w_up = lax.all_gather(up_weight, 'dp', axis=0, tiled=True)  44.1 us
    reduce_scatter x1, waiting for transfers between devices, local(): lax.psum_scatter(back_part, 'txt', scatter_dimension=0, tiled=True)  23.9 us
    reduce_scatter x1, waiting for transfers between devices, local(): lax.psum_scatter(normed_part, 'txt', scatter_dimension=1, tiled=True)  23.6 us
    reduce_scatter x1, waiting for transfers between devices, local(): mixed = lax.psum_scatter(mixed_part, 'txt', scatter_dimension=1, tiled=True)  22.2 us
    reduce_scatter x1, waiting for transfers between devices, local(): lax.psum_scatter(emb_part, 'txt', scatter_dimension=0, tiled=True)  21.7 us
    all_gather x1, blocking collectives, local(): gathered = lax.all_gather(resid, 'txt', axis=1, tiled=True)  8.89 us
    all_gather x1, blocking collectives, local(): lax.all_gather(output_gradient.astype(jnp.bfloat16), 'txt', axis=1, tiled...  6.85 us
  transfers between devices with their start and end apart: 6, of which 6 were waited for; matrix products, arithmetic and copies ran while one was open for 2% of the time, Pallas kernels for 0%

commit v1 on v0

--- a/solution.py
+++ b/solution.py
@@ -30,7 +30,11 @@
     input_inverse_deviation = lax.rsqrt(var_in + 1e-05)
     centered_input = (input_rows - input_mean) * input_inverse_deviation
     normed_input = (centered_input * prenorm_gain + prenorm_bias).astype(jnp.bfloat16)
-    w_up = lax.all_gather(up_weight, "dp", axis=0, tiled=True)
+    views = []
+    for _ in range(lax.axis_size("dp")):
+        views.append(up_weight)
+    work_now = lax.all_to_all(jnp.stack(views), axis_name="dp", split_axis=0, concat_axis=0)
+    w_up = jnp.concatenate(work_now, axis=0)
     w_down = lax.all_gather(down_weight, "dp", axis=1, tiled=True)
     pre_act = jnp.dot(normed_input, w_up, preferred_element_type=jnp.float32) + up_bias
     gate_sig = jax.nn.sigmoid(1.702 * pre_act)

time: 298 us -> 283 us (0.950)
  waiting for transfers between devices: 185 us -> 161 us
  starting transfers between devices: 0.2 us -> 7.62 us
    all_to_all x0 -> x1, waiting for transfers between devices: none -> 55.8 us  [local(): lax.all_to_all(jnp.stack(views), axis_name='dp', split_axis=0, concat_axi...]
    all_gather x1 -> x0, waiting for transfers between devices: 44.1 us -> none  [local(): w_up = lax.all_gather(up_weight, 'dp', axis=0, tiled=True)]
    all_gather x1, waiting for transfers between devices: 48.5 us -> 11.4 us  [local(): w_down = lax.all_gather(down_weight, 'dp', axis=1, tiled=True)]
    all_to_all x0 -> x1, starting transfers between devices: none -> 7.42 us  [local(): lax.all_to_all(jnp.stack(views), axis_name='dp', split_axis=0, concat_axi...]
where the time goes in v1:
time: 283 us; the launch traced here: 282 us
  waiting for transfers between devices  161 us (57%)
  blocking collectives  62.6 us (22%)
  matrix products  18.8 us (7%)
  other arithmetic  14.7 us (5%)
  between operations  14 us (5%)
  starting transfers between devices  7.62 us (3%)
  local copies, waits for them, and re-layouts  3.58 us (1%)
    all_to_all x1, waiting for transfers between devices, local(): lax.all_to_all(jnp.stack(views), axis_name='dp', split_axis=0, concat_axi...  55.8 us
    reduce_scatter x1, waiting for transfers between devices, local(): lax.psum_scatter(normed_part, 'txt', scatter_dimension=1, tiled=True)  24.3 us
    reduce_scatter x1, waiting for transfers between devices, local(): lax.psum_scatter(back_part, 'txt', scatter_dimension=0, tiled=True)  23.9 us
    reduce_scatter x1, waiting for transfers between devices, local(): mixed = lax.psum_scatter(mixed_part, 'txt', scatter_dimension=1, tiled=True)  23.1 us
    reduce_scatter x1, waiting for transfers between devices, local(): lax.psum_scatter(emb_part, 'txt', scatter_dimension=0, tiled=True)  21.7 us
    all_gather x1, waiting for transfers between devices, local(): w_down = lax.all_gather(down_weight, 'dp', axis=1, tiled=True)  11.4 us
    all_to_all x1, starting transfers between devices, local(): lax.all_to_all(jnp.stack(views), axis_name='dp', split_axis=0, concat_axi...  7.42 us
    all_gather x1, blocking collectives, local(): lax.all_gather(output_gradient.astype(jnp.bfloat16), 'txt', axis=1, tiled...  7.29 us
  transfers between devices with their start and end apart: 6, of which 6 were waited for; matrix products, arithmetic and copies ran while one was open for 2% of the time, Pallas kernels for 0%

profile of v1, /device:TPU:0, one launch (start us, length us, event | category | flops | bytes accessed | tf_op | source)
XLA Modules:
  0.0 282.2 jit_solution(11454266367679624674)
XLA Ops:
  6.5 2.6 stack.2
  9.1 7.4 %all-to-all-start = ((bf16[8,128,1024]{2,1,0:T(8,128)(2,1)}), bf16[8,128,1024]{2,1,0:T(8,128)(2,1)S(1)}, u32[]{:S(2)}, u32[]{:S(2)}) async-start(bf16[8,128,1024]{2,1,0:T(8,128)(2,1)} %stack.2), calls=%async_computation | async-start | bytes 4194304 | tf_op jit(solution)/shard_map/all_to_all | solution.py:36
  17.3 7.2 %all_gather.15 = bf16[256,1024]{1,0:T(8,128)(2,1)S(1)} all-gather(bf16[256,256]{1,0:T(8,128)(2,1)S(1)} %copy-done.6), channel_id=1, replica_groups=mesh['dp'=8,'txt'=4] {'txt'}, dimensions={1}, use_global_device_ids=true | all-gather | bytes 655360 | tf_op jit(solution)/shard_map/all_gather | solution.py:26
  24.8 55.8 %all-to-all-done = bf16[8,128,1024]{2,1,0:T(8,128)(2,1)S(1)} async-done(((bf16[8,128,1024]{2,1,0:T(8,128)(2,1)}), bf16[8,128,1024]{2,1,0:T(8,128)(2,1)S(1)}, u32[]{:S(2)}, u32[]{:S(2)}) %all-to-all-start) | async-done | bytes 2097184 | tf_op jit(solution)/shard_map/all_to_all | solution.py:36
  80.6 1.8 convolution_add_fusion
  82.4 11.4 %all-gather.2.cloned.1.call-done = bf16[1024,1024]{1,0:T(8,128)(2,1)} async-done(((bf16[1024,128]{1,0:T(8,128)(2,1)}), bf16[1024,1024]{1,0:T(8,128)(2,1)}) %all-gather.2.cloned.1.call-update) | async-done | bytes 2097168 | tf_op jit(solution)/shard_map/all_gather | solution.py:38
  93.8 3.6 %fusion.17 = f32[256,1024]{1,0:T(8,128)} fusion(bf16[1024,1024]{1,0:T(8,128)(2,1)} %all-gather.2.cloned.1.call-done, f32[256,1024]{1,0:T(8,128)} %convolution_add_fusion), kind=kOutput, calls=%fused_computation.32 | convolution fusion | flops 538443776 | bytes 4194304 | tf_op jit(solution)/shard_map/dot_general | solution.py:42
  98.4 23.1 %reduce-scatter.5.cloned.1.call-done = f32[256,256]{1,0:T(8,128)} async-done(((f32[256,1024]{1,0:T(8,128)}), f32[256,256]{1,0:T(8,128)}) %reduce-scatter.5.cloned.1.call-update) | async-done | bytes 262160 | tf_op jit(solution)/shard_map/reduce_scatter | solution.py:43
  121.5 1.1 fusion.38
  122.6 5.8 %all-reduce.2 = (f32[256]{0:T(256)S(1)}, f32[256]{0:T(256)S(1)}) all-reduce(f32[256]{0:T(256)S(1)} %get-tuple-element.12, f32[256]{0:T(256)S(1)} %get-tuple-element.11), channel_id=1, replica_groups=mesh['dp'=8,'txt'=4] {'txt'}, use_global_device_ids=true, to_apply=%region_6.0 | all-reduce | flops 512 | bytes 4096 | tf_op jit(solution)/shard_map/psum | solution.py:46
  128.4 1.2 fusion.25
  130.2 1.7 fusion.1
  132.0 21.7 %reduce-scatter.7.cloned.1.call-done = f32[64,768]{1,0:T(8,128)} async-done(((f32[256,768]{1,0:T(8,128)}), f32[64,768]{1,0:T(8,128)}) %reduce-scatter.7.cloned.1.call-update) | async-done | bytes 196624 | tf_op jit(solution)/shard_map/reduce_scatter | solution.py:53
  153.7 1.0 multiply_reduce_fusion.6
  155.7 6.1 %all_gather.17 = bf16[256,768]{1,0:T(8,128)(2,1)S(1)} all-gather(bf16[64,768]{1,0:T(8,128)(2,1)S(1)} %fusion.35), channel_id=1, replica_groups=mesh['dp'=8,'txt'=4] {'txt'}, dimensions={0}, use_global_device_ids=true | all-gather | bytes 491520 | tf_op jit(solution)/shard_map/all_gather | solution.py:56
  161.9 3.5 %fusion.41 = (f32[256]{0:T(256)S(1)}, f32[256,1280]{1,0:T(8,128)}) fusion(bf16[256,768]{1,0:T(8,128)(2,1)S(1)} %all_gather.17, bf16[1280,768]{1,0:T(8,128)(2,1)} %fusion.1), kind=kOutput, calls=%fused_computation.81 | convolution fusion | flops 503971584 | bytes 3671040 | tf_op jit(solution)/shard_map/ie,je->ij/dot_general | solution.py:61
  165.4 6.4 %pmax.7 = f32[256]{0:T(256)S(1)} all-reduce(f32[256]{0:T(256)S(1)} %get-tuple-element.28), channel_id=1, replica_groups=mesh['dp'=8,'txt'=4] {'txt'}, use_global_device_ids=true, to_apply=%region_11.0 | all-reduce | flops 256 | bytes 2048 | tf_op jit(solution)/shard_map/pmax | solution.py:65
  171.8 1.6 fusion.3
  173.4 5.7 %psum.58 = f32[256]{0:T(256)S(1)} all-reduce(f32[256]{0:T(256)S(1)} %fusion.3), channel_id=1, replica_groups=mesh['dp'=8,'txt'=4] {'txt'}, use_global_device_ids=true, to_apply=%region_13.0 | all-reduce | flops 256 | bytes 2048 | tf_op jit(solution)/shard_map/psum | solution.py:67
  179.1 3.2 %fusion.12 = f32[256,768]{1,0:T(8,128)} fusion(bf16[1280,768]{1,0:T(8,128)(2,1)S(1)} %copy-done.2, f32[256,1280]{1,0:T(8,128)} %get-tuple-element.29, s32[256]{0:T(256)S(1)} %broadcast_subtract_fusion, f32[256]{0:T(256)S(1)} %psum.58, f32[256]{0:T(256)S(1)} %pmax.7), kind=kOutput, calls=%fused_computation.27 | convolution fusion | flops 505610240 | bytes 4066304 | tf_op jit(solution)/shard_map/dot_general | solution.py:73
  182.3 23.9 %reduce-scatter.9.cloned.1.call-done = f32[64,768]{1,0:T(8,128)} async-done(((f32[256,768]{1,0:T(8,128)}), f32[64,768]{1,0:T(8,128)}) %reduce-scatter.9.cloned.1.call-update) | async-done | bytes 196624 | tf_op jit(solution)/shard_map/reduce_scatter | solution.py:74
  206.3 1.1 multiply_reduce_fusion.5
  208.5 6.3 %all_gather.18 = bf16[256,768]{1,0:T(8,128)(2,1)S(1)} all-gather(bf16[64,768]{1,0:T(8,128)(2,1)S(1)} %divide_convert_fusion), channel_id=1, replica_groups=mesh['dp'=8,'txt'=4] {'txt'}, dimensions={0}, use_global_device_ids=true | all-gather | bytes 491520 | tf_op jit(solution)/shard_map/all_gather | solution.py:77
  215.8 6.4 %all-reduce.1 = (f32[256]{0:T(256)S(1)}, f32[256]{0:T(256)S(1)}) all-reduce(f32[256]{0:T(256)S(1)} %get-tuple-element.10, f32[256]{0:T(256)S(1)} %get-tuple-element.9), channel_id=1, replica_groups=mesh['dp'=8,'txt'=4] {'txt'}, use_global_device_ids=true, to_apply=%region_19.0 | all-reduce | flops 512 | bytes 4096 | tf_op jit(solution)/shard_map/psum | solution.py:80
  222.2 1.9 fusion.39
  224.0 7.3 %all_gather.19 = bf16[256,1024]{1,0:T(8,128)(2,1)} all-gather(bf16[256,256]{1,0:T(8,128)(2,1)S(1)} %get-tuple-element.21), channel_id=1, replica_groups=mesh['dp'=8,'txt'=4] {'txt'}, dimensions={1}, use_global_device_ids=true | all-gather | bytes 655360 | tf_op jit(solution)/shard_map/all_gather | solution.py:84
  231.3 4.5 %fusion.4 = f32[256,1024]{1,0:T(8,128)} fusion(bf16[1024,1024]{1,0:T(8,128)(2,1)S(1)} %bitcast.15, bf16[256,1024]{1,0:T(8,128)(2,1)} %all_gather.19, bf16[1024,1024]{1,0:T(8,128)(2,1)} %all-gather.2.cloned.1.call-done, f32[256,1024]{1,0:T(8,128)} %convolution_add_fusion), kind=kOutput, calls=%fused_computation.16 | convolution fusion | flops 1076363264 | bytes 6815744 | tf_op jit(solution)/shard_map/if,df->id/dot_general | solution.py:89
  236.8 24.3 %reduce-scatter.11.cloned.1.call-done = f32[256,256]{1,0:T(8,128)} async-done(((f32[256,1024]{1,0:T(8,128)}), f32[256,256]{1,0:T(8,128)}) %reduce-scatter.11.cloned.1.call-update) | async-done | bytes 262160 | tf_op jit(solution)/shard_map/reduce_scatter | solution.py:90
  261.1 1.1 multiply_reduce_fusion.4
  262.2 5.8 %all-reduce = (f32[256]{0:T(256)S(1)}, f32[256]{0:T(256)S(1)}) all-reduce(f32[256]{0:T(256)S(1)} %get-tuple-element.8, f32[256]{0:T(256)S(1)} %get-tuple-element.7), channel_id=1, replica_groups=mesh['dp'=8,'txt'=4] {'txt'}, use_global_device_ids=true, to_apply=%region_24.0 | all-reduce | flops 512 | bytes 4096 | tf_op jit(solution)/shard_map/psum | solution.py:97
  268.0 1.2 multiply_reduce_fusion
  269.2 5.7 %psum.63 = f32[256]{0:T(256)S(1)} all-reduce(f32[256]{0:T(256)S(1)} %get-tuple-element.19), channel_id=1, replica_groups=mesh['dp'=8,'txt'=4] {'txt'}, use_global_device_ids=true, to_apply=%region_26.0 | all-reduce | flops 256 | bytes 2048 | tf_op jit(solution)/shard_map/psum | solution.py:110
  (56 shorter events, 6.9 us)
Async XLA Ops:
  6.5 121.9 %copy-start = (bf16[256,768]{1,0:T(8,128)(2,1)S(1)}, bf16[256,768]{1,0:T(8,128)(2,1)}, u32[]{:S(2)}) copy-start(bf16[256,768]{1,0:T(8,128)(2,1)} %param.22) | copy-start | bytes 1179652
  9.1 8.2 %copy-start.6 = (bf16[256,256]{1,0:T(8,128)(2,1)S(1)}, bf16[256,256]{1,0:T(8,128)(2,1)}, u32[]{:S(2)}) copy-start(bf16[256,256]{1,0:T(8,128)(2,1)} %param.13) | copy-start | bytes 393220
  9.1 71.5 %copy-start.11 = (f32[1024]{0:T(1024)S(1)}, f32[1024]{0:T(1024)}, u32[]{:S(2)}) copy-start(f32[1024]{0:T(1024)} %param.14) | copy-start | bytes 12292
  9.1 71.5 %copy-start.12 = (f32[1024]{0:T(1024)S(1)}, f32[1024]{0:T(1024)}, u32[]{:S(2)}) copy-start(f32[1024]{0:T(1024)} %param.17) | copy-start | bytes 12292
  9.1 71.5 %copy-start.13 = (f32[1024]{0:T(1024)S(1)}, f32[1024]{0:T(1024)}, u32[]{:S(2)}) copy-start(f32[1024]{0:T(1024)} %param.15) | copy-start | bytes 12292
  9.1 71.5 %all-to-all-start = ((bf16[8,128,1024]{2,1,0:T(8,128)(2,1)}), bf16[8,128,1024]{2,1,0:T(8,128)(2,1)S(1)}, u32[]{:S(2)}, u32[]{:S(2)}) async-start(bf16[8,128,1024]{2,1,0:T(8,128)(2,1)} %stack.2), calls=%async_computation | async-start | bytes 4194304 | tf_op jit(solution)/shard_map/all_to_all | solution.py:36
  16.5 77.3 %all-gather.2.cloned.1.call-start = ((), (), s32[]{:S(2)}) async-start(), calls=%async_computation.5 | async-start | bytes 2359296 | tf_op jit(solution)/shard_map/all_gather | solution.py:38
  17.3 104.3 %reduce-scatter.5.cloned.1.call-start = ((), (), s32[]{:S(2)}) async-start(), calls=%async_computation.6 | async-start | bytes 1310720 | tf_op jit(solution)/shard_map/reduce_scatter | solution.py:43
  80.6 1.8 copy-start.4
  82.4 46.0 %copy-start.8 = (f32[256]{0:T(256)S(1)}, f32[256]{0:T(256)}, u32[]{:S(2)}) copy-start(f32[256]{0:T(256)} %param.20) | copy-start | bytes 3076
  82.4 46.0 %copy-start.10 = (f32[256]{0:T(256)S(1)}, f32[256]{0:T(256)}, u32[]{:S(2)}) copy-start(f32[256]{0:T(256)} %param.21) | copy-start | bytes 3076
  97.4 32.3 %copy-start.9 = (s32[256]{0:T(256)S(1)}, s32[256]{0:T(256)}, u32[]{:S(2)}) copy-start(s32[256]{0:T(256)} %param.24) | copy-start | bytes 3076
  97.4 32.3 %copy-start.1 = (bf16[1280,768]{1,0:T(8,128)(2,1)S(1)}, bf16[1280,768]{1,0:T(8,128)(2,1)}, u32[]{:S(2)}) copy-start(bf16[1280,768]{1,0:T(8,128)(2,1)} %param.23) | copy-start | bytes 5898244
  97.5 56.2 %reduce-scatter.7.cloned.1.call-start = ((), (), s32[]{:S(2)}) async-start(), calls=%async_computation.7 | async-start | bytes 983040 | tf_op jit(solution)/shard_map/reduce_scatter | solution.py:53
  129.7 76.6 %reduce-scatter.9.cloned.1.call-start = ((), (), s32[]{:S(2)}) async-start(), calls=%async_computation.8 | async-start | bytes 983040 | tf_op jit(solution)/shard_map/reduce_scatter | solution.py:74
  161.9 17.2 %copy-start.2 = (bf16[1280,768]{1,0:T(8,128)(2,1)S(1)}, bf16[1280,768]{1,0:T(8,128)(2,1)}, u32[]{:S(2)}) copy-start(bf16[1280,768]{1,0:T(8,128)(2,1)} %fusion.1) | copy-start | bytes 5898244
  179.1 27.2 %copy-start.3 = (f32[64,768]{1,0:T(8,128)S(1)}, f32[64,768]{1,0:T(8,128)}, u32[]{:S(2)}) copy-start(f32[64,768]{1,0:T(8,128)} %reduce-scatter.7.cloned.1.call-done) | copy-start | bytes 589828
  182.3 78.8 %reduce-scatter.11.cloned.1.call-start = ((), (), s32[]{:S(2)}) async-start(), calls=%async_computation.9 | async-start | bytes 1310720 | tf_op jit(solution)/shard_map/reduce_scatter | solution.py:90
  208.4 22.9 %copy-start.5 = (bf16[8,128,1024]{2,1,0:T(8,128)(2,1)S(1)}, bf16[8,128,1024]{2,1,0:T(8,128)(2,1)}, u32[]{:S(2)}) copy-start(bf16[8,128,1024]{2,1,0:T(8,128)(2,1)} %copy-done.4) | copy-start | bytes 6291460
  235.8 32.1 %copy-start.7 = (f32[256,256]{1,0:T(8,128)S(1)}, f32[256,256]{1,0:T(8,128)}, u32[]{:S(2)}) copy-start(f32[256,256]{1,0:T(8,128)} %get-tuple-element.22) | copy-start | bytes 786436
Sparse Core Ops, SparseCore 0:
  19.4 74.3 all-gather.1
  97.6 23.9 reduce-scatter.4
  129.8 23.8 reduce-scatter.6
  182.4 23.8 reduce-scatter.8
  236.0 25.0 reduce-scatter.10
